TPU v7x, 32 devices: a whole 2x2x4 slice. The times are simulated.
32 devices in a mesh: band: 2 (over x), vis: 16 (over z, y, core).
Axes of the slice: x: 2, y: 2, z: 4, core: 2. Of those that a mesh axis runs over, the one named last changes fastest.
Arguments:
- sky_image: float32 [4096, 4096], P(('band', 'vis')), as said below
- coef_dual: float32 [4, 2048, 2048], P(None, ('band', 'vis')), may hold values from -12 to 12
- vis_dual: float32 [2, 16, 16, 4, 2, 32], P('band', 'vis'), may hold values from -12 to 12
- visibilities: float32 [2, 16, 16, 4, 2, 32], P('band', 'vis')
- kernel_blocks: bfloat16 [2, 16, 16, 4, 2, 32, 256], P('band', 'vis'), may hold values from -0.375 to 0.375
- tile_rows: int32 [2, 16, 16, 4], P('band', 'vis'), may hold values from 0 to 2047
- tile_counts: int32 [2, 16, 16], P('band', 'vis'), may hold values from 1 to 4, as said below
Outputs:
- new_image: float32 [4096, 4096], P(('band', 'vis'))
- new_coef_dual: float32 [4, 2048, 2048], P(None, ('band', 'vis'))
- new_vis_dual: float32 [2, 16, 16, 4, 2, 32], P('band', 'vis')
Inputs may be any that keep to these rules, and one draw needn't show every extreme that they name: `sky_image`: nonnegative. `tile_counts`: in every band some owner q has all 4 slots live from every device of that band.
All inputs are finite; a program needn't handle non-finite values.
Results may differ from a plain program's by a relative error of at most 0.0018.
Values may be sent and summed in bfloat16 or wider, within the bound.
A program may use at most 128 MiB of HBM per device.

v0:
```python
import math
import jax
import jax.numpy as jnp
from jax import lax
from jax.sharding import PartitionSpec as P

IMG = 4096
low_taps = (
    -0.010597401784997278,
    0.032883011666982945,
    0.030841381835986965,
    -0.18703481171888114,
    -0.02798376941698385,
    0.6308807679295904,
    0.7148465705525415,
    0.23037781330885523,
)
high_taps = tuple(((-1.0) ** offset * low_taps[7 - offset] for offset in range(8)))
highest = lax.Precision.HIGHEST


def shifted(block, axis, distance):
    devices = range(lax.axis_size(axis))
    route = [((i - distance) % len(devices), i) for i in devices]
    return lax.ppermute(block, axis, route)


def dft_table(table_size, sign):
    positions = jnp.arange(table_size, dtype=jnp.int32)
    phase = positions[:, None] * positions[None, :] % table_size
    angle = 2.0 * math.pi / table_size * phase.astype(jnp.float32)
    return (jnp.cos(angle), sign * jnp.sin(angle))


def section_one(table, values):
    return jnp.einsum("kn,...nm->...km", table, values, precision=highest)


def section_two(table, values):
    return jnp.einsum("qm,...km->...qk", table, values, precision=highest)


def dft_last(real_in, imag_in, sign):
    leading = real_in.shape[:-1]
    length = real_in.shape[-1]
    inner_len = 64
    outer_len = length // inner_len
    split_real = real_in.reshape(leading + (outer_len, inner_len))
    table_real, table_imag = dft_table(outer_len, sign)
    first_real = section_one(table_real, split_real)
    first_imag = section_one(table_imag, split_real)
    if imag_in is not None:
        split_imag = imag_in.reshape(leading + (outer_len, inner_len))
        first_real = first_real - section_one(table_imag, split_imag)
        first_imag = first_imag + section_one(table_real, split_imag)
    outer_index = jnp.arange(outer_len, dtype=jnp.int32)
    inner_index = jnp.arange(inner_len, dtype=jnp.int32)
    twist_phase = outer_index[:, None] * inner_index[None, :] % length
    twist_angle = 2.0 * math.pi / length * twist_phase.astype(jnp.float32)
    twist_real = jnp.cos(twist_angle)
    twist_imag = sign * jnp.sin(twist_angle)
    mid_real = first_real * twist_real - first_imag * twist_imag
    mid_imag = first_real * twist_imag + first_imag * twist_real
    last_real, last_imag = dft_table(inner_len, sign)
    out_real = section_two(last_real, mid_real) - section_two(last_imag, mid_imag)
    out_imag = section_two(last_real, mid_imag) + section_two(last_imag, mid_real)
    factor = 1.0 / math.sqrt(length)
    return (
        (out_real * factor).reshape(leading + (length,)),
        (out_imag * factor).reshape(leading + (length,)),
    )


def pieces_from_image(extrap, band_count, group_count):
    rows_dev = extrap.shape[0]
    image_width = extrap.shape[1]
    stripe = image_width // band_count
    piece_cols = stripe // group_count
    piece_rows = image_width // group_count
    col_real, col_imag = dft_last(extrap, None, -1.0)
    shaped = jnp.stack([col_real, col_imag]).reshape(
        2, 1, 1, rows_dev, band_count, group_count, piece_cols
    )
    moved = lax.all_to_all(
        lax.all_to_all(shaped, "band", split_axis=4, concat_axis=1, tiled=True),
        "vis",
        split_axis=5,
        concat_axis=2,
        tiled=True,
    )
    columns = jnp.transpose(moved.reshape(2, image_width, piece_cols), (2, 0, 1))
    row_real, row_imag = dft_last(columns[:, 0], columns[:, 1], -1.0)
    stacked = (
        jnp.stack([row_real, row_imag], axis=1)
        .astype(jnp.bfloat16)
        .reshape(piece_cols, 2, group_count, piece_rows)
    )
    pieces = lax.all_to_all(stacked, "vis", split_axis=2, concat_axis=0, tiled=True)
    return pieces.reshape(stripe, 2, piece_rows)


def image_from_pieces(piece_sum, band_count, group_count):
    stripe = piece_sum.shape[0]
    piece_rows = piece_sum.shape[2]
    piece_cols = stripe // group_count
    image_width = piece_rows * group_count
    rows_dev = image_width // (band_count * group_count)
    spread = lax.all_to_all(
        piece_sum.reshape(stripe, 2, 1, piece_rows), "vis", split_axis=0, concat_axis=2, tiled=True
    )
    spread = spread.reshape(piece_cols, 2, image_width)
    col_real, col_imag = dft_last(spread[:, 0], spread[:, 1], 1.0)
    stacked = jnp.transpose(jnp.stack([col_real, col_imag]), (0, 2, 1))
    shaped = stacked.reshape(2, band_count, group_count, rows_dev, 1, 1, piece_cols)
    moved = lax.all_to_all(
        lax.all_to_all(shaped, "band", split_axis=1, concat_axis=4, tiled=True),
        "vis",
        split_axis=2,
        concat_axis=5,
        tiled=True,
    )
    moved = moved.reshape(2, rows_dev, image_width)
    out_real, out_imag = dft_last(moved[0], moved[1], 1.0)
    return out_real


def cols_down(field):
    image_width = field.shape[1]
    extended = jnp.concatenate([field, field[:, :6]], axis=1)
    low_part = 0.0
    high_part = 0.0
    for offset in range(8):
        taken = extended[:, offset : offset + image_width : 2]
        low_part = low_part + low_taps[offset] * taken
        high_part = high_part + high_taps[offset] * taken
    return (low_part, high_part)


def cols_up(low_part, high_part):
    halves = []
    for parity in range(2):
        summed = 0.0
        for delay in range(4):
            summed = summed + low_taps[parity + 2 * delay] * jnp.roll(low_part, delay, axis=1)
            summed = summed + high_taps[parity + 2 * delay] * jnp.roll(high_part, delay, axis=1)
        halves.append(summed)
    return jnp.stack(halves, axis=2).reshape(low_part.shape[0], 2 * low_part.shape[1])


def rows_up(low_ext, high_ext, half_rows):
    halves = []
    for parity in range(2):
        summed = 0.0
        for delay in range(4):
            begin = 3 - delay
            summed = summed + low_taps[parity + 2 * delay] * low_ext[begin : begin + half_rows]
            summed = summed + high_taps[parity + 2 * delay] * high_ext[begin : begin + half_rows]
        halves.append(summed)
    return jnp.stack(halves, axis=1).reshape(2 * half_rows, low_ext.shape[1])


def analysis(extrap):
    rows_dev = extrap.shape[0]
    taken_rows = min(6, rows_dev)
    parts_list = [extrap]
    parts_list.append(shifted(extrap[:taken_rows], ("band", "vis"), -1))
    extended = jnp.concatenate(parts_list, axis=0)
    half_rows = rows_dev // 2
    rows_low = 0.0
    rows_high = 0.0
    for offset in range(8):
        taken = extended[offset : offset + 2 * half_rows : 2]
        rows_low = rows_low + low_taps[offset] * taken
        rows_high = rows_high + high_taps[offset] * taken
    low_low, low_high = cols_down(rows_low)
    high_low, high_high = cols_down(rows_high)
    return jnp.stack([low_low, low_high, high_low, high_high])


def synthesis(coef_dual):
    half_rows = coef_dual.shape[1]
    taken_rows = min(3, half_rows)
    parts_list = [shifted(coef_dual[:, half_rows - taken_rows :, :], ("band", "vis"), 1)]
    joined = jnp.concatenate(parts_list[::-1] + [coef_dual], axis=1)
    cols_low = rows_up(joined[0], joined[2], half_rows)
    cols_high = rows_up(joined[1], joined[3], half_rows)
    return cols_up(cols_low, cols_high)


def degrid(kernel_here, tiles):
    kernel_real = kernel_here[:, :, 0]
    kernel_imag = kernel_here[:, :, 1]
    tile_real = tiles[:, :, 0]
    tile_imag = tiles[:, :, 1]
    out_real = jnp.einsum(
        "qsat,qst->qsa", kernel_real, tile_real, preferred_element_type=jnp.float32
    ) - jnp.einsum("qsat,qst->qsa", kernel_imag, tile_imag, preferred_element_type=jnp.float32)
    out_imag = jnp.einsum(
        "qsat,qst->qsa", kernel_real, tile_imag, preferred_element_type=jnp.float32
    ) + jnp.einsum("qsat,qst->qsa", kernel_imag, tile_real, preferred_element_type=jnp.float32)
    return jnp.stack([out_real, out_imag], axis=2)


def grid_back(kernel_here, weights):
    kernel_real = kernel_here[:, :, 0]
    kernel_imag = kernel_here[:, :, 1]
    weight_real = weights[:, :, 0]
    weight_imag = weights[:, :, 1]
    grid_real = jnp.einsum(
        "qsat,qsa->qst", kernel_real, weight_real, preferred_element_type=jnp.float32
    ) + jnp.einsum("qsat,qsa->qst", kernel_imag, weight_imag, preferred_element_type=jnp.float32)
    grid_imag = jnp.einsum(
        "qsat,qsa->qst", kernel_real, weight_imag, preferred_element_type=jnp.float32
    ) - jnp.einsum("qsat,qsa->qst", kernel_imag, weight_real, preferred_element_type=jnp.float32)
    return jnp.stack([grid_real, grid_imag], axis=2)


def local(sky_image, coef_dual, vis_dual, visibilities, kernel_blocks, tile_rows, tile_counts):
    band_count = lax.axis_size("band")
    group_count = lax.axis_size("vis")
    kernel_here = kernel_blocks[0, 0]
    rows_here = tile_rows[0, 0]
    slot_count = rows_here.shape[1]
    live_slots = (
        jnp.arange(slot_count, dtype=jnp.int32)[None, :] < tile_counts[0, 0][:, None]
    ).astype(jnp.float32)[:, :, None, None]
    vis_data = visibilities[0, 0]
    vis_state = vis_dual[0, 0]
    image_width = sky_image.shape[1]
    stripe = image_width // band_count
    piece_rows = image_width // group_count
    incoming_rows = lax.all_to_all(rows_here, "vis", split_axis=0, concat_axis=0, tiled=True)
    data_part = jnp.sum(live_slots * vis_data * vis_data)
    weights = (live_slots * vis_state).astype(jnp.bfloat16)
    contrib = grid_back(kernel_here, weights)
    arrived = lax.all_to_all(contrib, "vis", split_axis=0, concat_axis=0, tiled=True)
    piece_sum = jax.ops.segment_sum(
        arrived.reshape(-1, 2, piece_rows), incoming_rows.reshape(-1), num_segments=stripe
    )
    adjoint_part = image_from_pieces(piece_sum, band_count, group_count)
    smooth = synthesis(coef_dual)
    new_image = jnp.maximum(sky_image - smooth - adjoint_part, 0.0)
    extrap = 2.0 * new_image - sky_image
    coeffs = analysis(extrap)
    abs_total = jnp.sum(jnp.abs(coeffs))
    coef_total = lax.psum(abs_total, ("band", "vis"))
    threshold = 0.5 * coef_total / (IMG * IMG)
    coef_dual = jnp.clip(coef_dual + coeffs, -threshold, threshold)
    piece_grid = pieces_from_image(extrap, band_count, group_count)
    tiles = lax.all_to_all(
        piece_grid[incoming_rows], "vis", split_axis=0, concat_axis=0, tiled=True
    )
    predicted = degrid(kernel_here, tiles)
    residual = live_slots * (vis_state + predicted - vis_data)
    resid_square = jnp.sum(residual * residual)
    norm_square, data_square = lax.psum((resid_square, data_part), ("band", "vis"))
    radius = 0.5 * jnp.sqrt(data_square + 1e-06)
    size_value = jnp.sqrt(norm_square + 1e-06)
    vis_state = residual * (1.0 - jnp.minimum(1.0, radius / size_value))
    return (new_image, coef_dual, vis_state[None, None])


def solution(mesh):
    return jax.shard_map(
        local,
        mesh=mesh,
        in_specs=(
            P(("band", "vis"), None),
            P(None, ("band", "vis"), None),
            P("band", "vis", None, None, None, None),
            P("band", "vis", None, None, None, None),
            P("band", "vis", None, None, None, None, None),
            P("band", "vis", None, None),
            P("band", "vis", None),
        ),
        out_specs=(
            P(("band", "vis"), None),
            P(None, ("band", "vis"), None),
            P("band", "vis", None, None, None, None),
        ),
        check_vma=False,
    )
```

profile of v0, /device:TPU:0, one launch (start us, length us, event | category | flops | bytes accessed | tf_op | source)
XLA Modules:
  0.0 1030.4 jit_solution(3161300191963925182)
XLA Ops:
  2.1 7.4 all-to-all-start
  15.9 5.8 all-to-all-start.1
  23.0 6.6 all-to-all-done.1
  32.6 7.0 scatter_fusion
  39.6 4.5 all-to-all-start.2
  44.6 77.0 %all-to-all-done.2 = f32[2048,2,1,256]{3,1,2,0:T(2,128)} async-done(((f32[2048,2,1,256]{3,1,2,0:T(2,128)}), f32[2048,2,1,256]{3,1,2,0:T(2,128)}, u32[]{:S(2)}, u32[]{:S(2)}) %all-to-all-start.2) | async-done | bytes 4194336 | tf_op jit(solution)/shard_map/all_to_all | solution.py:108
  121.6 4.6 copy.230
  126.2 5.8 copy.231
  144.5 4.5 fusion.7
  155.7 3.7 multiply_bitcast_fusion.4
  160.6 3.5 multiply_bitcast_fusion.3
  167.5 5.4 copy.244
  172.9 52.8 %all_to_all.118 = f32[2,2,16,128,1,1,128]{3,6,2,0,5,4,1:T(8,128)S(1)} all-to-all(f32[2,2,16,128,1,1,128]{3,6,2,0,5,4,1:T(8,128)} %copy.244), channel_id=1, replica_groups=mesh['band'=2,'vis'=16] {'band'}, dimensions={1} | all-to-all | bytes 8388608 | tf_op jit(solution)/shard_map/all_to_all | solution.py:116
  228.0 19.2 %all-to-all-start.4 = ((f32[2,1,16,128,2,1,128]{3,6,4,0,5,1,2:T(8,128)}), f32[2,1,16,128,2,1,128]{3,6,4,0,5,1,2:T(8,128)}, u32[]{:S(2)}, u32[]{:S(2)}) async-start(f32[2,1,16,128,2,1,128]{3,6,4,0,5,1,2:T(8,128)} %copy.245), calls=%async_computation.4 | async-start | bytes 8388608 | tf_op jit(solution)/shard_map/all_to_all | solution.py:115
  250.8 71.3 %collective-permute-done = f32[4,3,2048]{2,1,0:T(4,128)S(1)} collective-permute-done((f32[4,3,2048]{2,1,0:T(4,128)S(1)}, f32[4,3,2048]{2,1,0:T(4,128)S(1)}, u32[]{:S(2)}, u32[]{:S(2)}) %collective-permute-start) | collective-permute-done | bytes 98336 | tf_op jit(solution)/shard_map/ppermute | solution.py:25
  361.3 4.6 fusion.5
  376.5 3.8 fusion.39
  380.3 4.4 fusion.2
  388.1 3.5 fusion.29
  391.6 3.4 multiply_bitcast_fusion.1
  396.2 3.5 multiply_bitcast_fusion
  402.0 29.7 %all_to_all.119 = f32[2,1,1,128,2,16,128]{3,6,5,2,1,0,4:T(8,128)S(1)} all-to-all(f32[2,1,1,128,2,16,128]{3,6,5,2,1,0,4:T(8,128)S(1)} %copy.267), channel_id=1, replica_groups=mesh['band'=2,'vis'=16] {'band'}, dimensions={4} | all-to-all | bytes 8388608 | tf_op jit(solution)/shard_map/all_to_all | solution.py:85
  434.0 22.5 %all-to-all-start.6 = ((f32[2,2,1,128,1,16,128]{3,6,1,0,4,2,5:T(8,128)}), f32[2,2,1,128,1,16,128]{3,6,1,0,4,2,5:T(8,128)}, u32[]{:S(2)}, u32[]{:S(2)}) async-start(f32[2,2,1,128,1,16,128]{3,6,1,0,4,2,5:T(8,128)} %copy.268), calls=%async_computation.6 | async-start | bytes 8388608 | tf_op jit(solution)/shard_map/all_to_all | solution.py:84
  456.5 3.8 copy.257
  461.2 3.8 collective-permute-start.1
  465.0 41.1 %slice.319 = f32[64,4096]{0,1:T(8,128)} slice(f32[128,4096]{0,1:T(8,128)S(1)} %get-tuple-element.20), slice={[0:128:2], [0:4096:1]} | slice | bytes 2097152 | tf_op jit(solution)/shard_map/slice | solution.py:172
  509.0 17.5 %collective-permute-done.1 = f32[6,4096]{1,0:T(8,128)S(1)} collective-permute-done((f32[6,4096]{1,0:T(8,128)S(1)}, f32[6,4096]{1,0:T(8,128)S(1)}, u32[]{:S(2)}, u32[]{:S(2)}) %collective-permute-start.1) | collective-permute-done | bytes 98336 | tf_op jit(solution)/shard_map/ppermute | solution.py:25
  528.4 3.8 pad_maximum_fusion.1
  532.3 39.0 %slice.321 = f32[64,4096]{0,1:T(8,128)} slice(f32[134,4096]{0,1:T(8,128)} %pad_maximum_fusion.1), slice={[1:129:2], [0:4096:1]} | slice | bytes 2097152 | tf_op jit(solution)/shard_map/slice | solution.py:172
  571.2 39.0 %slice.322 = f32[64,4096]{0,1:T(8,128)} slice(f32[134,4096]{0,1:T(8,128)} %pad_maximum_fusion.1), slice={[2:130:2], [0:4096:1]} | slice | bytes 2097152 | tf_op jit(solution)/shard_map/slice | solution.py:172
  610.2 39.0 %slice.323 = f32[64,4096]{0,1:T(8,128)} slice(f32[134,4096]{0,1:T(8,128)} %pad_maximum_fusion.1), slice={[3:131:2], [0:4096:1]} | slice | bytes 2097152 | tf_op jit(solution)/shard_map/slice | solution.py:172
  649.2 39.0 %slice.324 = f32[64,4096]{0,1:T(8,128)} slice(f32[134,4096]{0,1:T(8,128)} %pad_maximum_fusion.1), slice={[4:132:2], [0:4096:1]} | slice | bytes 2097152 | tf_op jit(solution)/shard_map/slice | solution.py:172
  688.1 39.0 %slice.325 = f32[64,4096]{0,1:T(8,128)} slice(f32[134,4096]{0,1:T(8,128)} %pad_maximum_fusion.1), slice={[5:133:2], [0:4096:1]} | slice | bytes 2097152 | tf_op jit(solution)/shard_map/slice | solution.py:172
  727.1 39.0 %slice.326 = f32[64,4096]{0,1:T(8,128)} slice(f32[134,4096]{0,1:T(8,128)} %pad_maximum_fusion.1), slice={[6:134:2], [0:4096:1]} | slice | bytes 2097152 | tf_op jit(solution)/shard_map/slice | solution.py:172
  766.0 39.0 %slice.327 = f32[64,4096]{0,1:T(8,128)} slice(f32[134,4096]{0,1:T(8,128)} %pad_maximum_fusion.1), slice={[7:134:2], [0:4096:1]} | slice | bytes 2097152 | tf_op jit(solution)/shard_map/slice | solution.py:172
  805.0 5.5 copy.269
  823.0 4.8 fusion
  834.5 3.6 fusion.97
  838.8 3.5 fusion.100
  844.7 27.9 %all-to-all-start.7 = ((bf16[128,2,16,256]{0,3,1,2:T(8,128)(2,1)}), bf16[128,2,16,256]{0,3,1,2:T(8,128)(2,1)}, u32[]{:S(2)}, u32[]{:S(2)}) async-start(bf16[128,2,16,256]{0,3,1,2:T(8,128)(2,1)} %copy.280), calls=%async_computation.7 | async-start | bytes 4194304 | tf_op jit(solution)/shard_map/all_to_all | solution.py:98
  872.6 7.4 multiply_add_fusion.1
  882.4 3.5 slice.331
  885.9 3.4 slice.332
  889.3 3.5 slice.333
  892.8 3.5 slice.334
  896.3 3.5 slice.335
  899.7 3.5 slice.336
  903.2 6.2 slice.328
  911.8 3.5 slice.339
  915.3 3.5 slice.340
  918.8 3.4 slice.341
  922.2 3.5 slice.342
  925.7 3.4 slice.343
  929.2 3.5 slice.344
  932.6 3.5 slice.345
  936.1 6.2 slice.337
  942.4 4.4 add_bitcast_fusion.3
  950.0 3.9 copy.281
  953.9 5.8 copy.284
  962.6 6.0 all-to-all-start.8
  971.5 4.0 all-to-all-done.8
  980.6 38.1 %all-reduce = (f32[]{:T(128)}, f32[]{:T(128)}, f32[]{:T(128)}) all-reduce(f32[]{:T(128)} %abs_reduce_fusion, f32[]{:T(128)} %get-tuple-element.16, f32[]{:T(128)} %get-tuple-element.15), channel_id=1, replica_groups=mesh['band'=2,'vis'=16] {'band','vis'}, use_global_device_ids=true, to_apply=%region_2.3 | all-reduce | flops 3 | bytes 24 | tf_op jit(solution)/shard_map/psum | solution.py:246
  1020.6 5.0 maximum_minimum_fusion
  1025.7 3.8 copy.290
  (153 shorter events, 148.4 us)
Async XLA Ops:
  0.6 13.6 %copy-start.18 = (bf16[1,1,16,4,2,32,256]{6,5,4,3,2,1,0:T(8,128)(2,1)S(1)}, bf16[1,1,16,4,2,32,256]{6,5,4,3,2,1,0:T(8,128)(2,1)}, u32[]{:S(2)}) copy-start(bf16[1,1,16,4,2,32,256]{6,5,4,3,2,1,0:T(8,128)(2,1)} %param.11) | copy-start | bytes 6291460
  2.1 13.8 %all-to-all-start = ((s32[16,1,4]{2,1,0:T(1,128)}), s32[16,1,4]{2,1,0:T(1,128)S(1)}, u32[]{:S(2)}, u32[]{:S(2)}) async-start(s32[16,1,4]{2,1,0:T(1,128)} %copy.227), calls=%async_computation | async-start | bytes 16384 | tf_op jit(solution)/shard_map/all_to_all | solution.py:232
  10.3 1.0 copy-start.16
  15.9 13.7 %all-to-all-start.1 = ((f32[16,4,2,256]{3,2,1,0:T(2,128)}), f32[16,4,2,256]{3,2,1,0:T(2,128)S(1)}, u32[]{:S(2)}, u32[]{:S(2)}) async-start(f32[16,4,2,256]{3,2,1,0:T(2,128)} %pad_maximum_fusion.17), calls=%async_computation.1 | async-start | bytes 262144 | tf_op jit(solution)/shard_map/all_to_all | solution.py:236
  39.6 82.0 %all-to-all-start.2 = ((f32[2048,2,1,256]{3,1,2,0:T(2,128)}), f32[2048,2,1,256]{3,1,2,0:T(2,128)}, u32[]{:S(2)}, u32[]{:S(2)}) async-start(f32[2048,2,1,256]{3,1,2,0:T(2,128)} %bitcast.318), calls=%async_computation.2 | async-start | bytes 8388608 | tf_op jit(solution)/shard_map/all_to_all | solution.py:108
  228.0 19.2 %copy-start = (f32[4,64,2048]{2,1,0:T(8,128)S(1)}, f32[4,64,2048]{2,1,0:T(8,128)}, u32[]{:S(2)}) copy-start(f32[4,64,2048]{2,1,0:T(8,128)} %param.8) | copy-start | bytes 6291460
  228.0 120.3 %all-to-all-start.4 = ((f32[2,1,16,128,2,1,128]{3,6,4,0,5,1,2:T(8,128)}), f32[2,1,16,128,2,1,128]{3,6,4,0,5,1,2:T(8,128)}, u32[]{:S(2)}, u32[]{:S(2)}) async-start(f32[2,1,16,128,2,1,128]{3,6,4,0,5,1,2:T(8,128)} %copy.245), calls=%async_computation.4 | async-start | bytes 8388608 | tf_op jit(solution)/shard_map/all_to_all | solution.py:115
  247.3 74.8 %collective-permute-start = (f32[4,3,2048]{2,1,0:T(4,128)S(1)}, f32[4,3,2048]{2,1,0:T(4,128)S(1)}, u32[]{:S(2)}, u32[]{:S(2)}) collective-permute-start(f32[4,3,2048]{2,1,0:T(4,128)S(1)} %slice.284), channel_id=1, source_target_pairs={{31,0},{0,1},{1,2},{2,3},{3,4},{4,5},{5,6},{6,7},{7,8},{8,9},{9,10... | collective-permute-start | bytes 294920 | tf_op jit(solution)/shard_map/ppermute | solution.py:25
  342.2 1.7 copy-start.5
  372.6 1.6 copy-start.2
  372.6 2.2 copy-start.4
  434.0 371.0 %all-to-all-start.6 = ((f32[2,2,1,128,1,16,128]{3,6,1,0,4,2,5:T(8,128)}), f32[2,2,1,128,1,16,128]{3,6,1,0,4,2,5:T(8,128)}, u32[]{:S(2)}, u32[]{:S(2)}) async-start(f32[2,2,1,128,1,16,128]{3,6,1,0,4,2,5:T(8,128)} %copy.268), calls=%async_computation.6 | async-start | bytes 8388608 | tf_op jit(solution)/shard_map/all_to_all | solution.py:84
  461.2 65.2 %collective-permute-start.1 = (f32[6,4096]{1,0:T(8,128)S(1)}, f32[6,4096]{1,0:T(8,128)S(1)}, u32[]{:S(2)}, u32[]{:S(2)}) collective-permute-start(f32[6,4096]{1,0:T(8,128)S(1)} %copy.255), channel_id=1, source_target_pairs={{1,0},{2,1},{3,2},{4,3},{5,4},{6,5},{7,6},{8,7},{9,8},{10,9},{11,1... | collective-permute-start | bytes 294920 | tf_op jit(solution)/shard_map/ppermute | solution.py:25
  844.7 27.9 %copy-start.3 = (f32[64,4096]{0,1:T(8,128)S(1)}, f32[64,4096]{0,1:T(8,128)}, u32[]{:S(2)}) copy-start(f32[64,4096]{0,1:T(8,128)} %slice.319) | copy-start | bytes 3145732
  844.7 105.3 %all-to-all-start.7 = ((bf16[128,2,16,256]{0,3,1,2:T(8,128)(2,1)}), bf16[128,2,16,256]{0,3,1,2:T(8,128)(2,1)}, u32[]{:S(2)}, u32[]{:S(2)}) async-start(bf16[128,2,16,256]{0,3,1,2:T(8,128)(2,1)} %copy.280), calls=%async_computation.7 | async-start | bytes 4194304 | tf_op jit(solution)/shard_map/all_to_all | solution.py:98
  880.0 1.4 copy-start.1
  942.3 4.4 copy-start.6
  942.3 4.4 copy-start.7
  942.3 4.4 copy-start.8
  942.3 4.4 copy-start.9
  942.3 4.7 copy-start.10
  942.3 5.0 copy-start.11
  942.3 5.3 copy-start.12
  942.4 5.5 copy-start.13
  962.6 12.9 %all-to-all-start.8 = ((bf16[16,4,2,256]{3,2,1,0:T(2,128)(2,1)}), bf16[16,4,2,256]{3,2,1,0:T(2,128)(2,1)S(1)}, u32[]{:S(2)}, u32[]{:S(2)}) async-start(bf16[16,4,2,256]{3,2,1,0:T(2,128)(2,1)} %bitcast.95), calls=%async_computation.8 | async-start | bytes 131072 | tf_op jit(solution)/shard_map/all_to_all | solution.py:250
  975.5 3.5 copy-start.19
  977.3 2.5 copy-start.14
  977.3 2.5 copy-start.15
  977.3 2.5 copy-start.17
where the time goes:
time: 1040 us; the launch traced here: 1030 us
  local copies, waits for them, and re-layouts  472 us (45%)
  waiting for transfers between devices  177 us (17%)
  blocking collectives  121 us (12%)
  matrix products  108 us (10%)
  starting transfers between devices  97.5 us (9%)
  other arithmetic  51.8 us (5%)
    slice x8, local copies, waits for them, and re-layouts, analysis(): taken = extended[offset:offset + 2 * half_rows:2]  314 us
    ppermute x2, waiting for transfers between devices, shifted(): return lax.ppermute(block, axis, route)  88.9 us
    all_to_all x1, waiting for transfers between devices, image_from_pieces(): lax.all_to_all(piece_sum.reshape(stripe, 2, 1, piece_rows), 'vis', split_...  77 us
    slice x16, local copies, waits for them, and re-layouts, cols_down(): taken = extended[:, offset:offset + image_width:2]  58.4 us
    all_to_all x1, blocking collectives, image_from_pieces(): lax.all_to_all(shaped, 'band', split_axis=1, concat_axis=4, tiled=True)  52.8 us
    dot_general x14, matrix products, section_one(): return jnp.einsum('kn,...nm->...km', table, values, precision=highest)  51.9 us
    dot_general x14, matrix products, section_two(): return jnp.einsum('qm,...km->...qk', table, values, precision=highest)  48.1 us
    psum x1, blocking collectives, local(): coef_total = lax.psum(abs_total, ('band', 'vis'))  38.1 us
  transfers between devices with their start and end apart: 9, of which 6 were waited for; matrix products, arithmetic and copies ran while one was open for 43% of the time, Pallas kernels for 0%

commit v1 on v0

--- a/solution.py
+++ b/solution.py
@@ -81,12 +81,20 @@
     shaped = jnp.stack([col_real, col_imag]).reshape(
         2, 1, 1, rows_dev, band_count, group_count, piece_cols
     )
-    moved = lax.all_to_all(
-        lax.all_to_all(shaped, "band", split_axis=4, concat_axis=1, tiled=True),
-        "vis",
-        split_axis=5,
-        concat_axis=2,
-        tiled=True,
+    moved = jnp.concatenate(
+        lax.all_to_all(
+            jnp.stack(
+                jnp.split(
+                    lax.all_to_all(shaped, "band", split_axis=4, concat_axis=1, tiled=True),
+                    lax.axis_size("vis"),
+                    axis=5,
+                )
+            ),
+            "vis",
+            0,
+            0,
+        ),
+        axis=2,
     )
     columns = jnp.transpose(moved.reshape(2, image_width, piece_cols), (2, 0, 1))
     row_real, row_imag = dft_last(columns[:, 0], columns[:, 1], -1.0)

time: 1040 us -> 1050 us (level)
    unnamed x46 -> x61, local copies, waits for them, and re-layouts: 16.9 us -> 27.7 us
  transfers between devices with their start and end apart: 9 -> 9, of which waited for: 6 -> 6; matrix products, arithmetic and copies ran while one was open for 43% -> 42% of each run, Pallas kernels for 0% -> 0%
where the time goes in v1:
time: 1050 us; the launch traced here: 1040 us
  local copies, waits for them, and re-layouts  482 us (46%)
  waiting for transfers between devices  177 us (17%)
  blocking collectives  121 us (12%)
  matrix products  108 us (10%)
  starting transfers between devices  97.9 us (9%)
  other arithmetic  51.6 us (5%)
    slice x8, local copies, waits for them, and re-layouts, analysis(): taken = extended[offset:offset + 2 * half_rows:2]  314 us
    ppermute x2, waiting for transfers between devices, shifted(): return lax.ppermute(block, axis, route)  89.1 us
    all_to_all x1, waiting for transfers between devices, image_from_pieces(): lax.all_to_all(piece_sum.reshape(stripe, 2, 1, piece_rows), 'vis', split_...  77 us
    slice x16, local copies, waits for them, and re-layouts, cols_down(): taken = extended[:, offset:offset + image_width:2]  58.4 us
    all_to_all x1, blocking collectives, image_from_pieces(): lax.all_to_all(shaped, 'band', split_axis=1, concat_axis=4, tiled=True)  52.8 us
    dot_general x14, matrix products, section_one(): return jnp.einsum('kn,...nm->...km', table, values, precision=highest)  51.6 us
    dot_general x14, matrix products, section_two(): return jnp.einsum('qm,...km->...qk', table, values, precision=highest)  48.5 us
    psum x1, blocking collectives, local(): coef_total = lax.psum(abs_total, ('band', 'vis'))  38.1 us
  transfers between devices with their start and end apart: 9, of which 6 were waited for; matrix products, arithmetic and copies ran while one was open for 42% of the time, Pallas kernels for 0%

profile of v1, /device:TPU:0, one launch (start us, length us, event | category | flops | bytes accessed | tf_op | source)
XLA Modules:
  0.0 1040.1 jit_solution(16964855754754853718)
XLA Ops:
  2.1 7.4 all-to-all-start
  15.9 5.8 all-to-all-start.1
  23.0 6.6 all-to-all-done.1
  32.6 7.0 scatter_fusion
  39.6 4.5 all-to-all-start.2
  44.6 77.0 %all-to-all-done.2 = f32[2048,2,1,256]{3,1,2,0:T(2,128)} async-done(((f32[2048,2,1,256]{3,1,2,0:T(2,128)}), f32[2048,2,1,256]{3,1,2,0:T(2,128)}, u32[]{:S(2)}, u32[]{:S(2)}) %all-to-all-start.2) | async-done | bytes 4194336 | tf_op jit(solution)/shard_map/all_to_all | solution.py:116
  121.6 4.6 copy.376
  126.2 5.5 copy.377
  144.2 4.6 fusion.7
  155.4 3.9 multiply_bitcast_fusion.4
  160.5 3.5 multiply_bitcast_fusion.3
  167.5 5.4 copy.390
  172.8 52.8 %all_to_all.108 = f32[2,2,16,128,1,1,128]{3,6,2,0,5,4,1:T(8,128)S(1)} all-to-all(f32[2,2,16,128,1,1,128]{3,6,2,0,5,4,1:T(8,128)} %copy.390), channel_id=1, replica_groups=mesh['band'=2,'vis'=16] {'band'}, dimensions={1} | all-to-all | bytes 8388608 | tf_op jit(solution)/shard_map/all_to_all | solution.py:124
  228.0 19.2 %all-to-all-start.4 = ((f32[2,1,16,128,2,1,128]{3,6,4,0,5,1,2:T(8,128)}), f32[2,1,16,128,2,1,128]{3,6,4,0,5,1,2:T(8,128)}, u32[]{:S(2)}, u32[]{:S(2)}) async-start(f32[2,1,16,128,2,1,128]{3,6,4,0,5,1,2:T(8,128)} %copy.391), calls=%async_computation.4 | async-start | bytes 8388608 | tf_op jit(solution)/shard_map/all_to_all | solution.py:123
  250.8 71.3 %collective-permute-done = f32[4,3,2048]{2,1,0:T(4,128)S(1)} collective-permute-done((f32[4,3,2048]{2,1,0:T(4,128)S(1)}, f32[4,3,2048]{2,1,0:T(4,128)S(1)}, u32[]{:S(2)}, u32[]{:S(2)}) %collective-permute-start) | collective-permute-done | bytes 98336 | tf_op jit(solution)/shard_map/ppermute | solution.py:25
  361.0 4.7 fusion.5
  376.4 3.5 fusion.39
  379.9 4.4 fusion.2
  387.7 3.7 fusion.29
  391.4 3.4 multiply_bitcast_fusion.1
  396.1 3.5 multiply_bitcast_fusion
  401.9 29.7 %all_to_all.109 = f32[2,1,1,128,2,16,128]{3,6,5,2,1,0,4:T(8,128)S(1)} all-to-all(f32[2,1,1,128,2,16,128]{3,6,5,2,1,0,4:T(8,128)S(1)} %copy.413), channel_id=1, replica_groups=mesh['band'=2,'vis'=16] {'band'}, dimensions={4} | all-to-all | bytes 8388608 | tf_op jit(solution)/shard_map/all_to_all | solution.py:88
  443.1 5.5 copy.429
  448.6 22.7 %all-to-all-start.6 = ((f32[16,2,2,1,128,1,1,128]{7,4,2,1,6,5,3,0:T(8,128)}), f32[16,2,2,1,128,1,1,128]{7,4,2,1,6,5,3,0:T(8,128)}, u32[]{:S(2)}, u32[]{:S(2)}) async-start(f32[16,2,2,1,128,1,1,128]{7,4,2,1,6,5,3,0:T(8,128)} %copy.429), calls=%async_computation.6 | async-start | bytes 8388608 | tf_op jit(solution)/shard_map/all_to_all | solution.py:85
  471.3 3.8 copy.403
  476.0 3.9 collective-permute-start.1
  479.9 40.7 %slice.319 = f32[64,4096]{0,1:T(8,128)} slice(f32[128,4096]{0,1:T(8,128)S(1)} %get-tuple-element.23), slice={[0:128:2], [0:4096:1]} | slice | bytes 2097152 | tf_op jit(solution)/shard_map/slice | solution.py:180
  523.5 17.7 %collective-permute-done.1 = f32[6,4096]{1,0:T(8,128)S(1)} collective-permute-done((f32[6,4096]{1,0:T(8,128)S(1)}, f32[6,4096]{1,0:T(8,128)S(1)}, u32[]{:S(2)}, u32[]{:S(2)}) %collective-permute-start.1) | collective-permute-done | bytes 98336 | tf_op jit(solution)/shard_map/ppermute | solution.py:25
  543.2 3.8 pad_maximum_fusion.1
  547.0 39.0 %slice.321 = f32[64,4096]{0,1:T(8,128)} slice(f32[134,4096]{0,1:T(8,128)} %pad_maximum_fusion.1), slice={[1:129:2], [0:4096:1]} | slice | bytes 2097152 | tf_op jit(solution)/shard_map/slice | solution.py:180
  586.0 39.0 %slice.322 = f32[64,4096]{0,1:T(8,128)} slice(f32[134,4096]{0,1:T(8,128)} %pad_maximum_fusion.1), slice={[2:130:2], [0:4096:1]} | slice | bytes 2097152 | tf_op jit(solution)/shard_map/slice | solution.py:180
  624.9 39.0 %slice.323 = f32[64,4096]{0,1:T(8,128)} slice(f32[134,4096]{0,1:T(8,128)} %pad_maximum_fusion.1), slice={[3:131:2], [0:4096:1]} | slice | bytes 2097152 | tf_op jit(solution)/shard_map/slice | solution.py:180
  663.9 39.0 %slice.324 = f32[64,4096]{0,1:T(8,128)} slice(f32[134,4096]{0,1:T(8,128)} %pad_maximum_fusion.1), slice={[4:132:2], [0:4096:1]} | slice | bytes 2097152 | tf_op jit(solution)/shard_map/slice | solution.py:180
  702.8 39.0 %slice.325 = f32[64,4096]{0,1:T(8,128)} slice(f32[134,4096]{0,1:T(8,128)} %pad_maximum_fusion.1), slice={[5:133:2], [0:4096:1]} | slice | bytes 2097152 | tf_op jit(solution)/shard_map/slice | solution.py:180
  741.8 39.0 %slice.326 = f32[64,4096]{0,1:T(8,128)} slice(f32[134,4096]{0,1:T(8,128)} %pad_maximum_fusion.1), slice={[6:134:2], [0:4096:1]} | slice | bytes 2097152 | tf_op jit(solution)/shard_map/slice | solution.py:180
  780.8 39.4 %slice.327 = f32[64,4096]{0,1:T(8,128)} slice(f32[134,4096]{0,1:T(8,128)} %pad_maximum_fusion.1), slice={[7:134:2], [0:4096:1]} | slice | bytes 2097152 | tf_op jit(solution)/shard_map/slice | solution.py:180
  832.8 4.5 fusion
  844.0 3.7 fusion.97
  848.4 3.5 fusion.100
  854.3 27.9 %all-to-all-start.7 = ((bf16[128,2,16,256]{0,3,1,2:T(8,128)(2,1)}), bf16[128,2,16,256]{0,3,1,2:T(8,128)(2,1)}, u32[]{:S(2)}, u32[]{:S(2)}) async-start(bf16[128,2,16,256]{0,3,1,2:T(8,128)(2,1)} %copy.441), calls=%async_computation.7 | async-start | bytes 4194304 | tf_op jit(solution)/shard_map/all_to_all | solution.py:106
  882.2 7.4 multiply_add_fusion.1
  892.1 3.5 slice.331
  895.5 3.4 slice.332
  899.0 3.5 slice.333
  902.4 3.5 slice.334
  905.9 3.5 slice.335
  909.4 3.5 slice.336
  912.8 6.2 slice.328
  921.5 3.5 slice.339
  924.9 3.5 slice.340
  928.4 3.4 slice.341
  931.9 3.5 slice.342
  935.4 3.4 slice.343
  938.8 3.5 slice.344
  942.3 3.5 slice.345
  945.7 6.2 slice.337
  952.0 4.4 add_bitcast_fusion.3
  959.6 3.9 copy.442
  963.5 5.8 copy.445
  972.2 6.0 all-to-all-start.8
  981.1 4.0 all-to-all-done.8
  990.3 38.1 %all-reduce = (f32[]{:T(128)}, f32[]{:T(128)}, f32[]{:T(128)}) all-reduce(f32[]{:T(128)} %abs_reduce_fusion, f32[]{:T(128)} %get-tuple-element.19, f32[]{:T(128)} %get-tuple-element.18), channel_id=1, replica_groups=mesh['band'=2,'vis'=16] {'band','vis'}, use_global_device_ids=true, to_apply=%region_2.3 | all-reduce | flops 3 | bytes 24 | tf_op jit(solution)/shard_map/psum | solution.py:254
  1030.3 5.0 maximum_minimum_fusion
  1035.3 3.8 copy.451
  (169 shorter events, 157.7 us)
Async XLA Ops:
  0.6 13.6 %copy-start.18 = (bf16[1,1,16,4,2,32,256]{6,5,4,3,2,1,0:T(8,128)(2,1)S(1)}, bf16[1,1,16,4,2,32,256]{6,5,4,3,2,1,0:T(8,128)(2,1)}, u32[]{:S(2)}) copy-start(bf16[1,1,16,4,2,32,256]{6,5,4,3,2,1,0:T(8,128)(2,1)} %param.11) | copy-start | bytes 6291460
  2.1 13.8 %all-to-all-start = ((s32[16,1,4]{2,1,0:T(1,128)}), s32[16,1,4]{2,1,0:T(1,128)S(1)}, u32[]{:S(2)}, u32[]{:S(2)}) async-start(s32[16,1,4]{2,1,0:T(1,128)} %copy.373), calls=%async_computation | async-start | bytes 16384 | tf_op jit(solution)/shard_map/all_to_all | solution.py:240
  10.3 1.0 copy-start.16
  15.9 13.7 %all-to-all-start.1 = ((f32[16,4,2,256]{3,2,1,0:T(2,128)}), f32[16,4,2,256]{3,2,1,0:T(2,128)S(1)}, u32[]{:S(2)}, u32[]{:S(2)}) async-start(f32[16,4,2,256]{3,2,1,0:T(2,128)} %pad_maximum_fusion.17), calls=%async_computation.1 | async-start | bytes 262144 | tf_op jit(solution)/shard_map/all_to_all | solution.py:244
  39.6 82.0 %all-to-all-start.2 = ((f32[2048,2,1,256]{3,1,2,0:T(2,128)}), f32[2048,2,1,256]{3,1,2,0:T(2,128)}, u32[]{:S(2)}, u32[]{:S(2)}) async-start(f32[2048,2,1,256]{3,1,2,0:T(2,128)} %bitcast.410), calls=%async_computation.2 | async-start | bytes 8388608 | tf_op jit(solution)/shard_map/all_to_all | solution.py:116
  228.0 19.2 %copy-start = (f32[4,64,2048]{2,1,0:T(8,128)S(1)}, f32[4,64,2048]{2,1,0:T(8,128)}, u32[]{:S(2)}) copy-start(f32[4,64,2048]{2,1,0:T(8,128)} %param.8) | copy-start | bytes 6291460
  228.0 120.1 %all-to-all-start.4 = ((f32[2,1,16,128,2,1,128]{3,6,4,0,5,1,2:T(8,128)}), f32[2,1,16,128,2,1,128]{3,6,4,0,5,1,2:T(8,128)}, u32[]{:S(2)}, u32[]{:S(2)}) async-start(f32[2,1,16,128,2,1,128]{3,6,4,0,5,1,2:T(8,128)} %copy.391), calls=%async_computation.4 | async-start | bytes 8388608 | tf_op jit(solution)/shard_map/all_to_all | solution.py:123
  247.2 74.8 %collective-permute-start = (f32[4,3,2048]{2,1,0:T(4,128)S(1)}, f32[4,3,2048]{2,1,0:T(4,128)S(1)}, u32[]{:S(2)}, u32[]{:S(2)}) collective-permute-start(f32[4,3,2048]{2,1,0:T(4,128)S(1)} %slice.284), channel_id=1, source_target_pairs={{31,0},{0,1},{1,2},{2,3},{3,4},{4,5},{5,6},{6,7},{7,8},{8,9},{9,10... | collective-permute-start | bytes 294920 | tf_op jit(solution)/shard_map/ppermute | solution.py:25
  341.9 1.7 copy-start.5
  372.6 1.6 copy-start.2
  372.6 2.2 copy-start.4
  448.6 371.6 %all-to-all-start.6 = ((f32[16,2,2,1,128,1,1,128]{7,4,2,1,6,5,3,0:T(8,128)}), f32[16,2,2,1,128,1,1,128]{7,4,2,1,6,5,3,0:T(8,128)}, u32[]{:S(2)}, u32[]{:S(2)}) async-start(f32[16,2,2,1,128,1,1,128]{7,4,2,1,6,5,3,0:T(8,128)} %copy.429), calls=%async_computation.6 | async-start | bytes 8388608 | tf_op jit(solution)/shard_map/all_to_all | solution.py:85
  476.0 65.2 %collective-permute-start.1 = (f32[6,4096]{1,0:T(8,128)S(1)}, f32[6,4096]{1,0:T(8,128)S(1)}, u32[]{:S(2)}, u32[]{:S(2)}) collective-permute-start(f32[6,4096]{1,0:T(8,128)S(1)} %copy.401), channel_id=1, source_target_pairs={{1,0},{2,1},{3,2},{4,3},{5,4},{6,5},{7,6},{8,7},{9,8},{10,9},{11,1... | collective-permute-start | bytes 294920 | tf_op jit(solution)/shard_map/ppermute | solution.py:25
  854.3 27.9 %copy-start.3 = (f32[64,4096]{0,1:T(8,128)S(1)}, f32[64,4096]{0,1:T(8,128)}, u32[]{:S(2)}) copy-start(f32[64,4096]{0,1:T(8,128)} %slice.319) | copy-start | bytes 3145732
  854.3 105.3 %all-to-all-start.7 = ((bf16[128,2,16,256]{0,3,1,2:T(8,128)(2,1)}), bf16[128,2,16,256]{0,3,1,2:T(8,128)(2,1)}, u32[]{:S(2)}, u32[]{:S(2)}) async-start(bf16[128,2,16,256]{0,3,1,2:T(8,128)(2,1)} %copy.441), calls=%async_computation.7 | async-start | bytes 4194304 | tf_op jit(solution)/shard_map/all_to_all | solution.py:106
  889.6 1.4 copy-start.1
  951.9 4.4 copy-start.6
  952.0 4.4 copy-start.7
  952.0 4.4 copy-start.8
  952.0 4.4 copy-start.9
  952.0 4.7 copy-start.10
  952.0 5.0 copy-start.11
  952.0 5.3 copy-start.12
  952.0 5.5 copy-start.13
  972.2 12.9 %all-to-all-start.8 = ((bf16[16,4,2,256]{3,2,1,0:T(2,128)(2,1)}), bf16[16,4,2,256]{3,2,1,0:T(2,128)(2,1)S(1)}, u32[]{:S(2)}, u32[]{:S(2)}) async-start(bf16[16,4,2,256]{3,2,1,0:T(2,128)(2,1)} %bitcast.111), calls=%async_computation.8 | async-start | bytes 131072 | tf_op jit(solution)/shard_map/all_to_all | solution.py:258
  985.1 3.5 copy-start.19
  986.9 2.5 copy-start.14
  987.0 2.5 copy-start.15
  987.0 2.5 copy-start.17
